TPU v7x, 32 devices: a whole 2x2x4 slice. The times are simulated.
32 devices in a mesh: dp: 8 (over y, x, core), expert: 4 (over z).
Axes of the slice: x: 2, y: 2, z: 4, core: 2. Of those that a mesh axis runs over, the one named last changes fastest.
Arguments:
- policy_hidden: bfloat16 [1024, 4096], P('dp', 'expert'), may hold values from -6 to 6
- reference_hidden: bfloat16 [1024, 4096], P('dp', 'expert'), may hold values from -6 to 6
- policy_norm_gain: float32 [4096], P('expert'), may hold values from 0.25 to 1.75
- reference_norm_gain: float32 [4096], P('expert'), may hold values from 0.25 to 1.75
- policy_router: float32 [4096, 4], P('expert'), may hold values from -5.1875 to 5.1875
- reference_router: float32 [4096, 4], P('expert'), may hold values from -5.1875 to 5.1875
- policy_gate: bfloat16 [4, 4096, 8192], P('expert', 'dp'), may hold values from -0.09375 to 0.09375
- policy_up: bfloat16 [4, 4096, 8192], P('expert', 'dp'), may hold values from -0.09375 to 0.09375
- policy_down: bfloat16 [4, 8192, 4096], P('expert', 'dp'), may hold values from -0.0625 to 0.0625
- reference_gate: bfloat16 [4, 4096, 8192], P('expert', 'dp'), may hold values from -0.09375 to 0.09375
- reference_up: bfloat16 [4, 4096, 8192], P('expert', 'dp'), may hold values from -0.09375 to 0.09375
- reference_down: bfloat16 [4, 8192, 4096], P('expert', 'dp'), may hold values from -0.0625 to 0.0625
- expert_ids: int32 [1024, 2], P('dp'), may hold values from 0 to 3, all different within a row; in each aligned block of 128 rows (0 to 127, 128 to 255, ...) at most 96 rows name the same one
- lengths: int32 [32], P('dp'), may hold values from 1 to 32, as said below
Outputs:
- policy_mixture: bfloat16 [1024, 4096], P('dp', 'expert')
- reference_mixture: bfloat16 [1024, 4096], P('dp', 'expert')
- token_kl: float32 [1024], P('dp')
- loss: float32 [], replicated
Inputs may be any that keep to these rules, and one draw needn't show every extreme that they name: `expert_ids`: each row names 2 different experts; among the rows of one index of dp (aligned blocks of 128 rows) no expert is named more than 96 times, and in some block one expert is named exactly 96 times. The first lengths[r] of rollout r's 32 positions are live.
All inputs are finite; a program needn't handle non-finite values.
Results may differ from a plain program's by a relative error of at most 0.02.
Values may be sent and summed in bfloat16 or wider, within the bound.
A program may use at most 256 MiB of HBM per device.

v0:
```python
import jax
import jax.numpy as jnp
from jax import lax
from jax.sharding import PartitionSpec as P

D = 4096
SEG = 32
EPSILON = 1e-05
KL_WEIGHT = 1.0
BALANCE_WEIGHT = 0.5


def router_terms(hidden, norm_gain, router):
    values = hidden.astype(jnp.float32)
    partial_logits = jnp.dot(values * norm_gain, router, precision=lax.Precision.HIGHEST)
    return (partial_logits, jnp.sum(values * values, axis=1))


def expert_terms(piece_rows, weights):
    results = []
    for model_index in range(len(weights)):
        gate_weight, up_weight, down_weight = weights[model_index]
        model_rows = piece_rows[:, model_index, :]
        gate_value = jnp.dot(model_rows, gate_weight, preferred_element_type=jnp.float32)
        up_value = jnp.dot(model_rows, up_weight, preferred_element_type=jnp.float32)
        hidden = (jax.nn.silu(gate_value) * up_value).astype(jnp.bfloat16)
        results.append(jnp.dot(hidden, down_weight, preferred_element_type=jnp.float32))
    return jnp.stack(results, axis=1)


def mixture(slot_rows, weights):
    expert_count, slot_count, models, feature_block = slot_rows.shape
    model_width = expert_count * feature_block
    arrived_rows = lax.all_to_all(slot_rows, "expert", split_axis=0, concat_axis=3, tiled=True)
    local_rows = arrived_rows.reshape(slot_count, models, model_width)
    partial_terms = expert_terms(
        lax.all_gather(local_rows, "dp", axis=0, tiled=True), weights
    ).astype(jnp.bfloat16)
    summed = (
        lax.psum_scatter(partial_terms, "dp", scatter_dimension=0, tiled=True)
        .astype(jnp.float32)
        .astype(jnp.bfloat16)
    )
    result = lax.all_to_all(
        summed.reshape(1, slot_count, models, model_width),
        "expert",
        split_axis=3,
        concat_axis=0,
        tiled=True,
    )
    return result


def per_device(
    policy_hidden,
    reference_hidden,
    policy_norm_gain,
    reference_norm_gain,
    policy_router,
    reference_router,
    policy_gate,
    policy_up,
    policy_down,
    reference_gate,
    reference_up,
    reference_down,
    expert_ids,
    lengths,
):
    expert_count = lax.axis_size("expert")
    token_count, feature_block = policy_hidden.shape
    route_count = expert_ids.shape[1]
    slot_count = 3 * token_count // expert_count
    token_total = float(token_count * lax.axis_size("dp"))
    policy_partial, policy_squares = router_terms(policy_hidden, policy_norm_gain, policy_router)
    reference_partial, reference_squares = router_terms(
        reference_hidden, reference_norm_gain, reference_router
    )
    policy_partial, reference_partial, policy_squares, reference_squares = lax.psum(
        (policy_partial, reference_partial, policy_squares, reference_squares), "expert"
    )
    policy_scale = lax.rsqrt(policy_squares / D + EPSILON)[:, None]
    reference_scale = lax.rsqrt(reference_squares / D + EPSILON)[:, None]
    policy_logits = policy_partial * policy_scale
    reference_logits = reference_partial * reference_scale
    policy_rows = (policy_hidden.astype(jnp.float32) * policy_norm_gain * policy_scale).astype(
        jnp.bfloat16
    )
    reference_rows = (
        reference_hidden.astype(jnp.float32) * reference_norm_gain * reference_scale
    ).astype(jnp.bfloat16)
    live_mask = (
        (jnp.arange(SEG, dtype=jnp.int32)[None, :] < lengths[:, None])
        .reshape(-1)
        .astype(jnp.float32)
    )
    flat_ids = expert_ids.reshape(-1)
    onehot = (flat_ids[:, None] == jnp.arange(expert_count, dtype=jnp.int32)[None, :]).astype(
        jnp.int32
    )
    before = jnp.cumsum(onehot, axis=0) - onehot
    target = flat_ids * slot_count + jnp.sum(before * onehot, axis=1)
    slot_index = jnp.arange(expert_count * slot_count, dtype=jnp.int32)
    select = jnp.any(
        slot_index[:, None, None] == target.reshape(token_count, route_count)[None, :, :], axis=2
    ).astype(jnp.bfloat16)

    def pair_gates(logits):
        matches = expert_ids[:, :, None] == jnp.arange(expert_count, dtype=jnp.int32)[None, None, :]
        chosen = jnp.sum(jnp.where(matches, logits[:, None, :], 0.0), axis=2)
        return jax.nn.softmax(chosen, axis=1)

    def combine(expert_output, gates):
        picked = jnp.take(
            expert_output.reshape(expert_count * slot_count, feature_block), target, axis=0
        )
        picked = picked.reshape(token_count, route_count, feature_block).astype(jnp.float32)
        mixed_rows = jnp.sum(picked * gates[:, :, None], axis=1) * live_mask[:, None]
        return mixed_rows.astype(jnp.bfloat16)

    policy_gate_full, policy_up_full, reference_gate_full, reference_up_full = (
        lax.all_to_all(policy_gate, "dp", split_axis=2, concat_axis=1, tiled=True),
        lax.all_to_all(policy_up, "dp", split_axis=2, concat_axis=1, tiled=True),
        lax.all_to_all(reference_gate, "dp", split_axis=2, concat_axis=1, tiled=True),
        lax.all_to_all(reference_up, "dp", split_axis=2, concat_axis=1, tiled=True),
    )
    stacked_rows = jnp.concatenate((policy_rows, reference_rows), axis=1)
    placed = jnp.dot(select, stacked_rows, preferred_element_type=jnp.float32).astype(jnp.bfloat16)
    expert_output = mixture(
        placed.reshape(expert_count, slot_count, 2, feature_block),
        (
            (policy_gate_full[0], policy_up_full[0], policy_down[0]),
            (reference_gate_full[0], reference_up_full[0], reference_down[0]),
        ),
    )
    policy_output = expert_output[:, :, 0, :]
    reference_output = expert_output[:, :, 1, :]
    policy_mixture = combine(policy_output, pair_gates(policy_logits))
    reference_mixture = combine(reference_output, pair_gates(reference_logits))
    policy_logprob = jax.nn.log_softmax(policy_logits, axis=1)
    reference_logprob = jax.nn.log_softmax(reference_logits, axis=1)
    policy_prob = jnp.exp(policy_logprob)
    token_kl = jnp.sum(policy_prob * (policy_logprob - reference_logprob), axis=1) * live_mask
    route_onehot = onehot.reshape(token_count, route_count, expert_count)
    counts = jnp.sum(jnp.sum(route_onehot, axis=1).astype(jnp.float32) * live_mask[:, None], axis=0)
    probsum = jnp.sum(policy_prob * live_mask[:, None], axis=0)
    counts, probsum, kl_total = lax.psum((counts, probsum, jnp.sum(token_kl)), "dp")
    balance = expert_count * jnp.sum(counts / (route_count * token_total) * probsum / token_total)
    loss = KL_WEIGHT * kl_total / token_total + BALANCE_WEIGHT * balance
    return (policy_mixture, reference_mixture, token_kl, loss)


def solution(mesh):
    in_specs = (
        P("dp", "expert"),
        P("dp", "expert"),
        P("expert"),
        P("expert"),
        P("expert", None),
        P("expert", None),
        P("expert", "dp", None),
        P("expert", "dp", None),
        P("expert", "dp", None),
        P("expert", "dp", None),
        P("expert", "dp", None),
        P("expert", "dp", None),
        P("dp", None),
        P("dp"),
    )
    out_specs = (P("dp", "expert"), P("dp", "expert"), P("dp"), P())
    return jax.shard_map(
        per_device, mesh=mesh, in_specs=in_specs, out_specs=out_specs, check_vma=False
    )
```

profile of v0, /device:TPU:0, one launch (start us, length us, event | category | flops | bytes accessed | tf_op | source)
XLA Modules:
  0.0 886.3 jit_solution(8897518437984197567)
XLA Ops:
  13.4 14.3 %all-reduce.1 = (f32[128]{0:T(128)S(1)}, f32[128]{0:T(128)S(1)}, f32[128,4]{0,1:T(4,128)}, f32[128,4]{0,1:T(4,128)}) all-reduce(f32[128]{0:T(128)S(1)} %fusion.27, f32[128]{0:T(128)S(1)} %fusion.26, f32[128,4]{0,1:T(4,128)S(1)} %fusion.22, f32[128,4]{0,1:T(4,128)S(1)} %fusion.20), channel_id=1, replica_groups=mesh['dp'=8,'expert'=4] {'expert'}, use_global_device_ids=true, to_apply=%region_7.8 | all-reduce | flops 1280 | bytes 10240 | tf_op jit(solution)/shard_map/psum | solution.py:79
  39.5 34.5 %copy.109 = bf16[1,512,8192]{1,0,2:T(2,128)(2,1)} copy(bf16[1,512,8192]{2,1,0:T(8,128)(2,1)} %param.24) | data formatting | bytes 16777216 | tf_op args[7]
  74.5 54.6 %reduce.6 = bf16[8192,512]{1,0:T(8,128)(2,1)} reduce(bf16[8192,1,512]{2,1,0:T(2,128)(2,1)} %bitcast.98, bf16[]{:T(256)} %broadcast.143), dimensions={1}, to_apply=%bitcast.81.reduce_sub_computation | reduce | bytes 16777218
  145.4 34.5 %copy.107 = bf16[1,512,8192]{1,0,2:T(2,128)(2,1)} copy(bf16[1,512,8192]{2,1,0:T(8,128)(2,1)} %param.23) | data formatting | bytes 16777216 | tf_op args[6]
  180.0 54.6 %reduce.7 = bf16[8192,512]{1,0:T(8,128)(2,1)} reduce(bf16[8192,1,512]{2,1,0:T(2,128)(2,1)} %bitcast.100, bf16[]{:T(256)} %broadcast.143), dimensions={1}, to_apply=%bitcast.83.reduce_sub_computation | reduce | bytes 16777218
  254.4 34.7 %copy.113 = bf16[1,512,8192]{1,0,2:T(2,128)(2,1)} copy(bf16[1,512,8192]{2,1,0:T(8,128)(2,1)} %param.27) | data formatting | bytes 16777216 | tf_op args[10]
  289.2 54.6 %reduce.4 = bf16[8192,512]{1,0:T(8,128)(2,1)} reduce(bf16[8192,1,512]{2,1,0:T(2,128)(2,1)} %bitcast.101, bf16[]{:T(256)} %broadcast.143), dimensions={1}, to_apply=%bitcast.77.reduce_sub_computation | reduce | bytes 16777218
  354.9 36.7 %all-to-all-done.1 = bf16[8,2,262144]{2,1,0:T(2,128)(2,1)} async-done(((bf16[8,2,262144]{2,1,0:T(2,128)(2,1)}), bf16[8,2,262144]{2,1,0:T(2,128)(2,1)}, u32[]{:S(2)}, u32[]{:S(2)}) %all-to-all-start.1) | async-done | bytes 8388640 | tf_op jit(solution)/shard_map/all_to_all | solution.py:122
  397.0 34.5 %copy.111 = bf16[1,512,8192]{1,0,2:T(2,128)(2,1)} copy(bf16[1,512,8192]{2,1,0:T(8,128)(2,1)} %param.26) | data formatting | bytes 16777216 | tf_op args[9]
  431.5 54.6 %reduce.5 = bf16[8192,512]{1,0:T(8,128)(2,1)} reduce(bf16[8192,1,512]{2,1,0:T(2,128)(2,1)} %bitcast.99, bf16[]{:T(256)} %broadcast.143), dimensions={1}, to_apply=%bitcast.79.reduce_sub_computation | reduce | bytes 16777218
  502.3 13.3 %reshape.202 = bf16[8192,1,512]{2,1,0:T(2,128)(2,1)} reshape(bf16[8,2,262144]{2,1,0:T(2,128)(2,1)} %all-to-all-done.2) | data formatting | bytes 16777216
  515.6 11.6 %copy.120 = bf16[1,512,8192]{1,2,0:T(8,128)(2,1)} copy(bf16[1,512,8192]{1,0,2:T(2,128)(2,1)} %bitcast.94) | data formatting | bytes 16777216
  527.2 11.4 %copy.110 = bf16[1,8,512,1024]{3,2,1,0:T(8,128)(2,1)} copy(bf16[1,8,512,1024]{2,3,1,0:T(8,128)(2,1)} %bitcast.102) | data formatting | bytes 16777216 | tf_op jit(solution)/shard_map/all_to_all | solution.py:123
  538.7 13.3 %reshape.204 = bf16[8192,1,512]{2,1,0:T(2,128)(2,1)} reshape(bf16[8,2,262144]{2,1,0:T(2,128)(2,1)} %all-to-all-done.1) | data formatting | bytes 16777216
  552.0 11.6 %copy.119 = bf16[1,512,8192]{1,2,0:T(8,128)(2,1)} copy(bf16[1,512,8192]{1,0,2:T(2,128)(2,1)} %bitcast.95) | data formatting | bytes 16777216
  575.0 13.3 %reshape.198 = bf16[8192,1,512]{2,1,0:T(2,128)(2,1)} reshape(bf16[8,2,262144]{2,1,0:T(2,128)(2,1)} %all-to-all-done.4) | data formatting | bytes 16777216
  588.3 11.6 %copy.122 = bf16[1,512,8192]{1,2,0:T(8,128)(2,1)} copy(bf16[1,512,8192]{1,0,2:T(2,128)(2,1)} %bitcast.96) | data formatting | bytes 16777216
  600.0 11.5 %copy.114 = bf16[1,8,512,1024]{3,2,1,0:T(8,128)(2,1)} copy(bf16[1,8,512,1024]{2,3,1,0:T(8,128)(2,1)} %bitcast.104) | data formatting | bytes 16777216 | tf_op jit(solution)/shard_map/all_to_all | solution.py:125
  611.4 13.3 %reshape.200 = bf16[8192,1,512]{2,1,0:T(2,128)(2,1)} reshape(bf16[8,2,262144]{2,1,0:T(2,128)(2,1)} %all-to-all-done.3) | data formatting | bytes 16777216
  624.7 11.8 %copy.121 = bf16[1,512,8192]{1,2,0:T(8,128)(2,1)} copy(bf16[1,512,8192]{1,0,2:T(2,128)(2,1)} %bitcast.97) | data formatting | bytes 16777216
  636.6 11.5 %copy.112 = bf16[1,8,512,1024]{3,2,1,0:T(8,128)(2,1)} copy(bf16[1,8,512,1024]{2,3,1,0:T(8,128)(2,1)} %bitcast.105) | data formatting | bytes 16777216 | tf_op jit(solution)/shard_map/all_to_all | solution.py:124
  712.5 94.5 %reduce-scatter.2.cloned.1.call-done = bf16[96,2,4096]{2,0,1:T(8,128)(2,1)} async-done(((bf16[768,2,4096]{2,0,1:T(8,128)(2,1)}), bf16[96,2,4096]{2,0,1:T(8,128)(2,1)}) %reduce-scatter.2.cloned.1.call-update) | async-done | bytes 1572880 | tf_op jit(solution)/shard_map/reduce_scatter | solution.py:40
  818.9 13.4 %all-reduce = (f32[]{:T(128)}, f32[4]{0:T(128)S(1)}, f32[4]{0:T(128)S(1)}) all-reduce(f32[]{:T(128)} %get-tuple-element.18, f32[4]{0:T(128)S(1)} %get-tuple-element.6, f32[4]{0:T(128)S(1)} %get-tuple-element.10), channel_id=1, replica_groups=mesh['dp'=8,'expert'=4] {'dp'}, use_global_device_ids=true, to_apply=%region_23.26 | all-reduce | flops 9 | bytes 72 | tf_op jit(solution)/shard_map/psum | solution.py:147
  834.7 30.7 %all-to-all-done.5 = bf16[1,96,2,4096]{1,2,0,3:T(2,128)(2,1)S(1)} async-done(((bf16[1,96,2,4096]{1,2,0,3:T(2,128)(2,1)}), bf16[1,96,2,4096]{1,2,0,3:T(2,128)(2,1)S(1)}, u32[]{:S(2)}, u32[]{:S(2)}) %all-to-all-start.5) | async-done | bytes 1572896 | tf_op jit(solution)/shard_map/all_to_all | solution.py:44
  (136 shorter events, 188.6 us)
Async XLA Ops:
  8.3 24.2 %copy-start.3 = (s32[256]{0:T(256)}, s32[256]{0:T(256)S(1)}, u32[]{:S(2)}) copy-start(s32[256]{0:T(256)S(1)} %eq.60) | copy-start | bytes 3076
  31.5 42.5 %copy-start.5 = (s32[256]{0:T(256)}, s32[256]{0:T(256)S(1)}, u32[]{:S(2)}) copy-start(s32[256]{0:T(256)S(1)} %fusion.36) | copy-start | bytes 3076
  35.9 104.3 %all-to-all-start = ((bf16[4,96,2,1024]{3,1,2,0:T(8,128)(2,1)}), bf16[4,96,2,1024]{3,1,2,0:T(8,128)(2,1)S(1)}, u32[]{:S(2)}, u32[]{:S(2)}) async-start(bf16[4,96,2,1024]{3,1,2,0:T(8,128)(2,1)} %copy.105), calls=%async_computation | async-start | bytes 3145728 | tf_op jit(solution)/shard_map/all_to_all | solution.py:34
  140.2 105.5 %all-to-all-start.2 = ((bf16[8,2,262144]{2,1,0:T(2,128)(2,1)}), bf16[8,2,262144]{2,1,0:T(2,128)(2,1)}, u32[]{:S(2)}, u32[]{:S(2)}) async-start(bf16[8,2,262144]{2,1,0:T(2,128)(2,1)} %reshape.201), calls=%async_computation.2 | async-start | bytes 16777216 | tf_op jit(solution)/shard_map/all_to_all | solution.py:123
  245.8 145.8 %all-to-all-start.1 = ((bf16[8,2,262144]{2,1,0:T(2,128)(2,1)}), bf16[8,2,262144]{2,1,0:T(2,128)(2,1)}, u32[]{:S(2)}, u32[]{:S(2)}) async-start(bf16[8,2,262144]{2,1,0:T(2,128)(2,1)} %reshape.203), calls=%async_computation.1 | async-start | bytes 16777216 | tf_op jit(solution)/shard_map/all_to_all | solution.py:122
  250.7 397.3 %all-gather.2.cloned.1.call-start = ((), (), s32[]{:S(2)}) async-start(), calls=%async_computation.7 | async-start | bytes 14155776 | tf_op jit(solution)/shard_map/all_gather | solution.py:37
  391.6 105.7 %all-to-all-start.4 = ((bf16[8,2,262144]{2,1,0:T(2,128)(2,1)}), bf16[8,2,262144]{2,1,0:T(2,128)(2,1)}, u32[]{:S(2)}, u32[]{:S(2)}) async-start(bf16[8,2,262144]{2,1,0:T(2,128)(2,1)} %reshape.197), calls=%async_computation.4 | async-start | bytes 16777216 | tf_op jit(solution)/shard_map/all_to_all | solution.py:125
  497.3 114.2 %all-to-all-start.3 = ((bf16[8,2,262144]{2,1,0:T(2,128)(2,1)}), bf16[8,2,262144]{2,1,0:T(2,128)(2,1)}, u32[]{:S(2)}, u32[]{:S(2)}) async-start(bf16[8,2,262144]{2,1,0:T(2,128)(2,1)} %reshape.199), calls=%async_computation.3 | async-start | bytes 16777216 | tf_op jit(solution)/shard_map/all_to_all | solution.py:124
  502.2 304.8 %reduce-scatter.2.cloned.1.call-start = ((), (), s32[]{:S(2)}) async-start(), calls=%async_computation.8 | async-start | bytes 14155776 | tf_op jit(solution)/shard_map/reduce_scatter | solution.py:40
  648.0 11.0 %copy-start.13 = (bf16[768,2,4096]{2,0,1:T(8,128)(2,1)S(1)}, bf16[768,2,4096]{2,0,1:T(8,128)(2,1)}, u32[]{:S(2)}) copy-start(bf16[768,2,4096]{2,0,1:T(8,128)(2,1)} %all-gather.2.cloned.1.call-done) | copy-start | bytes 37748740
  659.1 20.4 %slice-start = ((s8[8388608]{0:T(1024)(128)(4,1)}), s8[4194304]{0:T(1024)(128)(4,1)S(1)}, s32[]{:S(2)}) async-start(s8[8388608]{0:T(1024)(128)(4,1)} %bitcast.111), calls=%async_computation.9 | async-start | bytes 8388608
  668.8 10.7 %slice-start.1 = ((s8[8388608]{0:T(1024)(128)(4,1)}), s8[4194304]{0:T(1024)(128)(4,1)S(1)}, s32[]{:S(2)}) async-start(s8[8388608]{0:T(1024)(128)(4,1)} %bitcast.111), calls=%async_computation.10 | async-start | bytes 8388608
  668.8 20.9 %slice-start.2 = ((s8[8388608]{0:T(1024)(128)(4,1)}), s8[4194304]{0:T(1024)(128)(4,1)S(1)}, s32[]{:S(2)}) async-start(s8[8388608]{0:T(1024)(128)(4,1)} %bitcast.114), calls=%async_computation.11 | async-start | bytes 8388608
  668.8 30.9 %slice-start.4 = ((s8[8388608]{0:T(1024)(128)(4,1)}), s8[4194304]{0:T(1024)(128)(4,1)S(1)}, s32[]{:S(2)}) async-start(s8[8388608]{0:T(1024)(128)(4,1)} %bitcast.121), calls=%async_computation.13 | async-start | bytes 8388608
  679.5 20.2 %slice-start.5 = ((s8[8388608]{0:T(1024)(128)(4,1)}), s8[4194304]{0:T(1024)(128)(4,1)S(1)}, s32[]{:S(2)}) async-start(s8[8388608]{0:T(1024)(128)(4,1)} %bitcast.121), calls=%async_computation.14 | async-start | bytes 8388608
  712.4 104.9 %copy-start.14 = (s32[4]{0:T(128)S(1)}, s32[4]{0:T(128)}, u32[]{:S(2)}) copy-start(s32[4]{0:T(128)} %param.30) | copy-start | bytes 52
  712.4 105.1 %copy-start.10 = (f32[128]{0:T(128)S(1)}, f32[128]{0:T(128)}, u32[]{:S(2)}) copy-start(f32[128]{0:T(128)} %copy-done.9) | copy-start | bytes 1540
  712.4 105.1 %copy-start.12 = (f32[128,4]{0,1:T(4,128)S(1)}, f32[128,4]{0,1:T(4,128)}, u32[]{:S(2)}) copy-start(f32[128,4]{0,1:T(4,128)} %get-tuple-element.16) | copy-start | bytes 6148
  712.4 105.1 %copy-start.8 = (f32[128]{0:T(128)S(1)}, f32[128]{0:T(128)}, u32[]{:S(2)}) copy-start(f32[128]{0:T(128)} %copy-done.7) | copy-start | bytes 1540
  712.4 105.1 %copy-start.11 = (f32[128,4]{0,1:T(4,128)S(1)}, f32[128,4]{0,1:T(4,128)}, u32[]{:S(2)}) copy-start(f32[128,4]{0,1:T(4,128)} %get-tuple-element.17) | copy-start | bytes 6148
  712.4 105.2 %copy-start.2 = (s32[128,2]{0,1:T(2,128)S(1)}, s32[128,2]{0,1:T(2,128)}, u32[]{:S(2)}) copy-start(s32[128,2]{0,1:T(2,128)} %param.29) | copy-start | bytes 3076
  712.4 122.2 %copy-start.4 = (s32[256]{0:T(256)S(1)}, s32[256]{0:T(256)}, u32[]{:S(2)}) copy-start(s32[256]{0:T(256)} %copy-done.3) | copy-start | bytes 3076
  712.5 122.2 %copy-start.6 = (s32[256]{0:T(256)S(1)}, s32[256]{0:T(256)}, u32[]{:S(2)}) copy-start(s32[256]{0:T(256)} %copy-done.5) | copy-start | bytes 3076
  812.7 52.6 %all-to-all-start.5 = ((bf16[1,96,2,4096]{1,2,0,3:T(2,128)(2,1)}), bf16[1,96,2,4096]{1,2,0,3:T(2,128)(2,1)S(1)}, u32[]{:S(2)}, u32[]{:S(2)}) async-start(bf16[1,96,2,4096]{1,2,0,3:T(2,128)(2,1)} %copy.115), calls=%async_computation.6 | async-start | bytes 4194304 | tf_op jit(solution)/shard_map/all_to_all | solution.py:44
  (5 other events, 23.0 us)
Sparse Core Ops, SparseCore 0:
  254.6 141.9 all-gather.1
  712.6 94.3 reduce-scatter.1
where the time goes:
time: 900 us; the launch traced here: 886 us
  local copies, waits for them, and re-layouts  352 us (39%)
  other arithmetic  236 us (26%)
  waiting for transfers between devices  162 us (18%)
  matrix products  62.3 us (7%)
  starting transfers between devices  28.7 us (3%)
  blocking collectives  27.7 us (3%)
  between operations  17.2 us (2%)
    unnamed x60, local copies, waits for them, and re-layouts  284 us
    unnamed x8, other arithmetic  218 us
    reduce_scatter x1, waiting for transfers between devices, mixture(): lax.psum_scatter(partial_terms, 'dp', scatter_dimension=0, tiled=True)  94.5 us
    all_to_all x1, waiting for transfers between devices, per_device(): lax.all_to_all(policy_gate, 'dp', split_axis=2, concat_axis=1, tiled=True)  36.7 us
    all_to_all x1, waiting for transfers between devices, mixture(): lax.all_to_all(summed.reshape(1, slot_count, models, model_width), 'exper...  30.7 us
    dot_general x2, matrix products, expert_terms(): jnp.dot(model_rows, up_weight, preferred_element_type=jnp.float32)  21.2 us
    dot_general x2, matrix products, expert_terms(): jnp.dot(model_rows, gate_weight, preferred_element_type=jnp.float32)  19.7 us
  transfers between devices with their start and end apart: 8, of which 3 were waited for; matrix products, arithmetic and copies ran while one was open for 62% of the time, Pallas kernels for 0%

commit v1 on v0

--- a/solution.py
+++ b/solution.py
@@ -8,6 +8,13 @@
 EPSILON = 1e-05
 KL_WEIGHT = 1.0
 BALANCE_WEIGHT = 0.5
+
+
+def trade_parts(x, axis, split, join):
+    peers = lax.axis_size(axis)
+    pieces = jnp.stack(jnp.split(x, peers, axis=split), axis=0)
+    pieces = lax.all_to_all(pieces, axis, split_axis=0, concat_axis=0)
+    return jnp.concatenate(pieces, axis=join)
 
 
 def router_terms(hidden, norm_gain, router):
@@ -119,7 +126,7 @@
         return mixed_rows.astype(jnp.bfloat16)
 
     policy_gate_full, policy_up_full, reference_gate_full, reference_up_full = (
-        lax.all_to_all(policy_gate, "dp", split_axis=2, concat_axis=1, tiled=True),
+        trade_parts(policy_gate, "dp", 2, 1),
         lax.all_to_all(policy_up, "dp", split_axis=2, concat_axis=1, tiled=True),
         lax.all_to_all(reference_gate, "dp", split_axis=2, concat_axis=1, tiled=True),
         lax.all_to_all(reference_up, "dp", split_axis=2, concat_axis=1, tiled=True),

time: 900 us -> 859 us (0.954)
  waiting for transfers between devices: 162 us -> 237 us
  local copies, waits for them, and re-layouts: 352 us -> 288 us
  other arithmetic: 236 us -> 182 us
    all_to_all x1, waiting for transfers between devices: 0.01 us -> 75.7 us  [per_device(): lax.all_to_all(policy_up, 'dp', split_axis=2, concat_axis=1, tiled=True)]
    unnamed x60 -> x59, local copies, waits for them, and re-layouts: 284 us -> 230 us
    unnamed x8 -> x6, other arithmetic: 218 us -> 164 us
    all_to_all x1, waiting for transfers between devices: 36.7 us -> 0.01 us  [trade_parts(): pieces = lax.all_to_all(pieces, axis, split_axis=0, concat_axis=0)]
    all_to_all x1, waiting for transfers between devices: 0.01 us -> 36.4 us  [per_device(): lax.all_to_all(reference_up, 'dp', split_axis=2, concat_axis=1, tiled=True)]
    all_to_all x1 -> x0, local copies, waits for them, and re-layouts: 11.4 us -> none  [per_device(): lax.all_to_all(policy_gate, 'dp', split_axis=2, concat_axis=1, tiled=True)]
  transfers between devices with their start and end apart: 8 -> 8, of which waited for: 3 -> 4; matrix products, arithmetic and copies ran while one was open for 62% -> 56% of each run, Pallas kernels for 0% -> 0%
where the time goes in v1:
time: 859 us; the launch traced here: 846 us
  local copies, waits for them, and re-layouts  288 us (34%)
  waiting for transfers between devices  237 us (28%)
  other arithmetic  182 us (21%)
  matrix products  65.8 us (8%)
  starting transfers between devices  28.5 us (3%)
  blocking collectives  27.7 us (3%)
  between operations  17.1 us (2%)
    unnamed x59, local copies, waits for them, and re-layouts  230 us
    unnamed x6, other arithmetic  164 us
    reduce_scatter x1, waiting for transfers between devices, mixture(): lax.psum_scatter(partial_terms, 'dp', scatter_dimension=0, tiled=True)  94.5 us
    all_to_all x1, waiting for transfers between devices, per_device(): lax.all_to_all(policy_up, 'dp', split_axis=2, concat_axis=1, tiled=True)  75.7 us
    all_to_all x1, waiting for transfers between devices, per_device(): lax.all_to_all(reference_up, 'dp', split_axis=2, concat_axis=1, tiled=True)  36.4 us
    all_to_all x1, waiting for transfers between devices, mixture(): lax.all_to_all(summed.reshape(1, slot_count, models, model_width), 'exper...  30.6 us
    dot_general x2, matrix products, expert_terms(): jnp.dot(hidden, down_weight, preferred_element_type=jnp.float32)  22.9 us
    dot_general x2, matrix products, expert_terms(): jnp.dot(model_rows, gate_weight, preferred_element_type=jnp.float32)  21.7 us
  transfers between devices with their start and end apart: 8, of which 4 were waited for; matrix products, arithmetic and copies ran while one was open for 56% of the time, Pallas kernels for 0%

profile of v1, /device:TPU:0, one launch (start us, length us, event | category | flops | bytes accessed | tf_op | source)
XLA Modules:
  0.0 846.2 jit_solution(1451613363071750666)
XLA Ops:
  13.4 14.3 %all-reduce.1 = (f32[128]{0:T(128)S(1)}, f32[128]{0:T(128)S(1)}, f32[128,4]{0,1:T(4,128)}, f32[128,4]{0,1:T(4,128)}) all-reduce(f32[128]{0:T(128)S(1)} %fusion.27, f32[128]{0:T(128)S(1)} %fusion.26, f32[128,4]{0,1:T(4,128)S(1)} %fusion.22, f32[128,4]{0,1:T(4,128)S(1)} %fusion.20), channel_id=1, replica_groups=mesh['dp'=8,'expert'=4] {'expert'}, use_global_device_ids=true, to_apply=%region_7.8 | all-reduce | flops 1280 | bytes 10240 | tf_op jit(solution)/shard_map/psum | solution.py:86
  39.5 34.5 %copy.105 = bf16[1,512,8192]{1,0,2:T(2,128)(2,1)} copy(bf16[1,512,8192]{2,1,0:T(8,128)(2,1)} %param.27) | data formatting | bytes 16777216 | tf_op args[10]
  74.5 54.6 %reduce.4 = bf16[8192,512]{1,0:T(8,128)(2,1)} reduce(bf16[8192,1,512]{2,1,0:T(2,128)(2,1)} %bitcast.108, bf16[]{:T(256)} %broadcast.143), dimensions={1}, to_apply=%bitcast.90.reduce_sub_computation | reduce | bytes 16777218
  149.2 34.7 %copy.103 = bf16[1,512,8192]{1,0,2:T(2,128)(2,1)} copy(bf16[1,512,8192]{2,1,0:T(8,128)(2,1)} %param.26) | data formatting | bytes 16777216 | tf_op args[9]
  183.9 54.6 %reduce.5 = bf16[8192,512]{1,0:T(8,128)(2,1)} reduce(bf16[8192,1,512]{2,1,0:T(2,128)(2,1)} %bitcast.110, bf16[]{:T(256)} %broadcast.143), dimensions={1}, to_apply=%bitcast.92.reduce_sub_computation | reduce | bytes 16777218
  238.5 11.2 %reshape.198 = bf16[8,2,262144]{2,1,0:T(2,128)(2,1)} reshape(bf16[8192,512]{1,0:T(8,128)(2,1)} %reduce.5) | data formatting | bytes 16777216
  249.7 36.4 %all-to-all-done.4 = bf16[8,2,262144]{2,1,0:T(2,128)(2,1)} async-done(((bf16[8,2,262144]{2,1,0:T(2,128)(2,1)}), bf16[8,2,262144]{2,1,0:T(2,128)(2,1)}, u32[]{:S(2)}, u32[]{:S(2)}) %all-to-all-start.4) | async-done | bytes 8388640 | tf_op jit(solution)/shard_map/all_to_all | solution.py:132
  291.0 34.5 %copy.101 = bf16[1,512,8192]{1,0,2:T(2,128)(2,1)} copy(bf16[1,512,8192]{2,1,0:T(8,128)(2,1)} %param.24) | data formatting | bytes 16777216 | tf_op args[7]
  325.6 54.6 %reduce.6 = bf16[8192,512]{1,0:T(8,128)(2,1)} reduce(bf16[8192,1,512]{2,1,0:T(2,128)(2,1)} %bitcast.109, bf16[]{:T(256)} %broadcast.143), dimensions={1}, to_apply=%bitcast.94.reduce_sub_computation | reduce | bytes 16777218
  414.6 75.7 %all-to-all-done.2 = bf16[8,2,262144]{2,1,0:T(2,128)(2,1)} async-done(((bf16[8,2,262144]{2,1,0:T(2,128)(2,1)}), bf16[8,2,262144]{2,1,0:T(2,128)(2,1)}, u32[]{:S(2)}, u32[]{:S(2)}) %all-to-all-start.2) | async-done | bytes 8388640 | tf_op jit(solution)/shard_map/all_to_all | solution.py:130
  495.5 13.3 %reshape.197 = bf16[8192,1,512]{2,1,0:T(2,128)(2,1)} reshape(bf16[8,2,262144]{2,1,0:T(2,128)(2,1)} %all-to-all-done.4) | data formatting | bytes 16777216
  508.8 11.6 %copy.113 = bf16[1,512,8192]{1,2,0:T(8,128)(2,1)} copy(bf16[1,512,8192]{1,0,2:T(2,128)(2,1)} %bitcast.105) | data formatting | bytes 16777216
  520.5 11.4 %copy.106 = bf16[1,8,512,1024]{3,2,1,0:T(8,128)(2,1)} copy(bf16[1,8,512,1024]{2,3,1,0:T(8,128)(2,1)} %bitcast.111) | data formatting | bytes 16777216 | tf_op jit(solution)/shard_map/all_to_all | solution.py:132
  531.9 13.3 %reshape.199 = bf16[8192,1,512]{2,1,0:T(2,128)(2,1)} reshape(bf16[8,2,262144]{2,1,0:T(2,128)(2,1)} %all-to-all-done.3) | data formatting | bytes 16777216
  545.2 11.6 %copy.112 = bf16[1,512,8192]{1,2,0:T(8,128)(2,1)} copy(bf16[1,512,8192]{1,0,2:T(2,128)(2,1)} %bitcast.106) | data formatting | bytes 16777216
  556.9 11.4 %copy.104 = bf16[1,8,512,1024]{3,2,1,0:T(8,128)(2,1)} copy(bf16[1,8,512,1024]{2,3,1,0:T(8,128)(2,1)} %bitcast.112) | data formatting | bytes 16777216 | tf_op jit(solution)/shard_map/all_to_all | solution.py:131
  568.3 13.3 %reshape.201 = bf16[8192,1,512]{2,1,0:T(2,128)(2,1)} reshape(bf16[8,2,262144]{2,1,0:T(2,128)(2,1)} %all-to-all-done.2) | data formatting | bytes 16777216
  581.6 11.6 %copy.111 = bf16[1,512,8192]{1,2,0:T(8,128)(2,1)} copy(bf16[1,512,8192]{1,0,2:T(2,128)(2,1)} %bitcast.107) | data formatting | bytes 16777216
  593.2 11.4 %copy.102 = bf16[1,8,512,1024]{3,2,1,0:T(8,128)(2,1)} copy(bf16[1,8,512,1024]{2,3,1,0:T(8,128)(2,1)} %bitcast.113) | data formatting | bytes 16777216 | tf_op jit(solution)/shard_map/all_to_all | solution.py:130
  625.9 12.1 %fusion.10 = bf16[768,1,4096]{2,0,1:T(8,128)(2,1)} fusion(bf16[768,1024]{1,0:T(8,128)(2,1)S(1)} %multiply_convert_fusion, bf16[1,1024,4096]{2,1,0:T(8,128)(2,1)} %param.28), kind=kOutput, calls=%fused_computation.11 | convolution fusion | flops 6445596672 | bytes 16252928 | tf_op jit(solution)/shard_map/dot_general | solution.py:34
  644.7 11.5 %multiply_convert_fusion.1 = bf16[768,1024]{1,0:T(8,128)(2,1)S(1)} fusion(f32[768,1024]{1,0:T(8,128)S(1)} %fusion.16, bf16[4096,1024]{1,0:T(8,128)(2,1)} %bitcast.13, bf16[768,2,4096]{2,0,1:T(8,128)(2,1)} %all-gather.2.cloned.1.call-done), kind=kOutput, calls=%fused_computation.18 | convolution fusion | flops 6447169536 | bytes 19398656 | tf_op jit(solution)/shard_map/dot_general | solution.py:31
  672.6 94.5 %reduce-scatter.2.cloned.1.call-done = bf16[96,2,4096]{2,0,1:T(8,128)(2,1)} async-done(((bf16[768,2,4096]{2,0,1:T(8,128)(2,1)}), bf16[96,2,4096]{2,0,1:T(8,128)(2,1)}) %reduce-scatter.2.cloned.1.call-update) | async-done | bytes 1572880 | tf_op jit(solution)/shard_map/reduce_scatter | solution.py:47
  778.9 13.4 %all-reduce = (f32[]{:T(128)}, f32[4]{0:T(128)S(1)}, f32[4]{0:T(128)S(1)}) all-reduce(f32[]{:T(128)} %get-tuple-element.18, f32[4]{0:T(128)S(1)} %get-tuple-element.6, f32[4]{0:T(128)S(1)} %get-tuple-element.10), channel_id=1, replica_groups=mesh['dp'=8,'expert'=4] {'dp'}, use_global_device_ids=true, to_apply=%region_23.26 | all-reduce | flops 9 | bytes 72 | tf_op jit(solution)/shard_map/psum | solution.py:154
  794.7 30.6 %all-to-all-done.5 = bf16[1,96,2,4096]{1,2,0,3:T(2,128)(2,1)S(1)} async-done(((bf16[1,96,2,4096]{1,2,0,3:T(2,128)(2,1)}), bf16[1,96,2,4096]{1,2,0,3:T(2,128)(2,1)S(1)}, u32[]{:S(2)}, u32[]{:S(2)}) %all-to-all-start.5) | async-done | bytes 1572896 | tf_op jit(solution)/shard_map/all_to_all | solution.py:51
  (133 shorter events, 152.7 us)
Async XLA Ops:
  8.3 24.2 %copy-start.3 = (s32[256]{0:T(256)}, s32[256]{0:T(256)S(1)}, u32[]{:S(2)}) copy-start(s32[256]{0:T(256)S(1)} %eq.60) | copy-start | bytes 3076
  31.5 42.5 %copy-start.5 = (s32[256]{0:T(256)}, s32[256]{0:T(256)S(1)}, u32[]{:S(2)}) copy-start(s32[256]{0:T(256)S(1)} %fusion.36) | copy-start | bytes 3076
  35.9 104.3 %all-to-all-start = ((bf16[4,96,2,1024]{3,1,2,0:T(8,128)(2,1)}), bf16[4,96,2,1024]{3,1,2,0:T(8,128)(2,1)S(1)}, u32[]{:S(2)}, u32[]{:S(2)}) async-start(bf16[4,96,2,1024]{3,1,2,0:T(8,128)(2,1)} %copy.99), calls=%async_computation | async-start | bytes 3145728 | tf_op jit(solution)/shard_map/all_to_all | solution.py:41
  140.2 145.8 %all-to-all-start.4 = ((bf16[8,2,262144]{2,1,0:T(2,128)(2,1)}), bf16[8,2,262144]{2,1,0:T(2,128)(2,1)}, u32[]{:S(2)}, u32[]{:S(2)}) async-start(bf16[8,2,262144]{2,1,0:T(2,128)(2,1)} %reshape.196), calls=%async_computation.4 | async-start | bytes 16777216 | tf_op jit(solution)/shard_map/all_to_all | solution.py:132
  145.3 459.4 %all-gather.2.cloned.1.call-start = ((), (), s32[]{:S(2)}) async-start(), calls=%async_computation.7 | async-start | bytes 14155776 | tf_op jit(solution)/shard_map/all_gather | solution.py:44
  286.1 105.2 %all-to-all-start.3 = ((bf16[8,2,262144]{2,1,0:T(2,128)(2,1)}), bf16[8,2,262144]{2,1,0:T(2,128)(2,1)}, u32[]{:S(2)}, u32[]{:S(2)}) async-start(bf16[8,2,262144]{2,1,0:T(2,128)(2,1)} %reshape.198), calls=%async_computation.3 | async-start | bytes 16777216 | tf_op jit(solution)/shard_map/all_to_all | solution.py:131
  391.3 99.0 %all-to-all-start.2 = ((bf16[8,2,262144]{2,1,0:T(2,128)(2,1)}), bf16[8,2,262144]{2,1,0:T(2,128)(2,1)}, u32[]{:S(2)}, u32[]{:S(2)}) async-start(bf16[8,2,262144]{2,1,0:T(2,128)(2,1)} %reshape.200), calls=%async_computation.2 | async-start | bytes 16777216 | tf_op jit(solution)/shard_map/all_to_all | solution.py:130
  490.3 154.4 %all-to-all-start.1 = ((bf16[8,1,512,1024]{3,2,1,0:T(8,128)(2,1)}), bf16[8,1,512,1024]{3,2,1,0:T(8,128)(2,1)}, u32[]{:S(2)}, u32[]{:S(2)}) async-start(bf16[8,1,512,1024]{3,2,1,0:T(8,128)(2,1)} %bitcast_dynamic-update-slice_fusion), calls=%async_computation.1 | async-start | bytes 16777216 | tf_op jit(solution)/shard_map/all_to_all | solution.py:16
  495.5 271.5 %reduce-scatter.2.cloned.1.call-start = ((), (), s32[]{:S(2)}) async-start(), calls=%async_computation.8 | async-start | bytes 14155776 | tf_op jit(solution)/shard_map/reduce_scatter | solution.py:47
  604.7 11.0 %copy-start.13 = (bf16[768,2,4096]{2,0,1:T(8,128)(2,1)S(1)}, bf16[768,2,4096]{2,0,1:T(8,128)(2,1)}, u32[]{:S(2)}) copy-start(bf16[768,2,4096]{2,0,1:T(8,128)(2,1)} %all-gather.2.cloned.1.call-done) | copy-start | bytes 37748740
  615.7 22.3 %slice-start = ((s8[8388608]{0:T(1024)(128)(4,1)}), s8[4194304]{0:T(1024)(128)(4,1)S(1)}, s32[]{:S(2)}) async-start(s8[8388608]{0:T(1024)(128)(4,1)} %bitcast.119), calls=%async_computation.9 | async-start | bytes 8388608
  625.9 12.1 %slice-start.1 = ((s8[8388608]{0:T(1024)(128)(4,1)}), s8[4194304]{0:T(1024)(128)(4,1)S(1)}, s32[]{:S(2)}) async-start(s8[8388608]{0:T(1024)(128)(4,1)} %bitcast.119), calls=%async_computation.10 | async-start | bytes 8388608
  644.7 22.3 %slice-start.2 = ((s8[6291456]{0:T(1024)(128)(4,1)}), s8[2097152]{0:T(1024)(128)(4,1)S(1)}, s32[]{:S(2)}) async-start(s8[6291456]{0:T(1024)(128)(4,1)} %bitcast.124), calls=%async_computation.11 | async-start | bytes 4194304
  656.2 10.8 %slice-start.3 = ((s8[6291456]{0:T(1024)(128)(4,1)}), s8[4194304]{0:T(1024)(128)(4,1)S(1)}, s32[]{:S(2)}) async-start(s8[6291456]{0:T(1024)(128)(4,1)} %bitcast.124), calls=%async_computation.12 | async-start | bytes 8388608
  672.5 104.8 %copy-start.14 = (s32[4]{0:T(128)S(1)}, s32[4]{0:T(128)}, u32[]{:S(2)}) copy-start(s32[4]{0:T(128)} %param.30) | copy-start | bytes 52
  672.5 105.0 %copy-start.10 = (f32[128]{0:T(128)S(1)}, f32[128]{0:T(128)}, u32[]{:S(2)}) copy-start(f32[128]{0:T(128)} %copy-done.9) | copy-start | bytes 1540
  672.5 105.0 %copy-start.12 = (f32[128,4]{0,1:T(4,128)S(1)}, f32[128,4]{0,1:T(4,128)}, u32[]{:S(2)}) copy-start(f32[128,4]{0,1:T(4,128)} %get-tuple-element.16) | copy-start | bytes 6148
  672.5 105.1 %copy-start.8 = (f32[128]{0:T(128)S(1)}, f32[128]{0:T(128)}, u32[]{:S(2)}) copy-start(f32[128]{0:T(128)} %copy-done.7) | copy-start | bytes 1540
  672.5 105.1 %copy-start.11 = (f32[128,4]{0,1:T(4,128)S(1)}, f32[128,4]{0,1:T(4,128)}, u32[]{:S(2)}) copy-start(f32[128,4]{0,1:T(4,128)} %get-tuple-element.17) | copy-start | bytes 6148
  672.5 105.1 %copy-start.2 = (s32[128,2]{0,1:T(2,128)S(1)}, s32[128,2]{0,1:T(2,128)}, u32[]{:S(2)}) copy-start(s32[128,2]{0,1:T(2,128)} %param.29) | copy-start | bytes 3076
  672.5 122.1 %copy-start.4 = (s32[256]{0:T(256)S(1)}, s32[256]{0:T(256)}, u32[]{:S(2)}) copy-start(s32[256]{0:T(256)} %copy-done.3) | copy-start | bytes 3076
  672.5 122.1 %copy-start.6 = (s32[256]{0:T(256)S(1)}, s32[256]{0:T(256)}, u32[]{:S(2)}) copy-start(s32[256]{0:T(256)} %copy-done.5) | copy-start | bytes 3076
  772.7 52.6 %all-to-all-start.5 = ((bf16[1,96,2,4096]{1,2,0,3:T(2,128)(2,1)}), bf16[1,96,2,4096]{1,2,0,3:T(2,128)(2,1)S(1)}, u32[]{:S(2)}, u32[]{:S(2)}) async-start(bf16[1,96,2,4096]{1,2,0,3:T(2,128)(2,1)} %copy.107), calls=%async_computation.6 | async-start | bytes 4194304 | tf_op jit(solution)/shard_map/all_to_all | solution.py:51
  831.8 6.3 copy-start.1
  (3 other events, 6.5 us)
Sparse Core Ops, SparseCore 0:
  149.3 141.7 all-gather.1
  672.7 94.2 reduce-scatter.1
